TPU v7x, 32 devices: a whole 2x2x4 slice. The times are simulated.
32 devices in a mesh: seq: 8 (over z, y), tp: 4 (over x, core).
Axes of the slice: x: 2, y: 2, z: 4, core: 2. Of those that a mesh axis runs over, the one named last changes fastest.
Arguments:
- ssm_inputs: bfloat16 [8192, 8192], P('seq', 'tp'), may hold values from -6 to 6
- step_sizes: float32 [8192, 128], P('seq', 'tp'), as said below
- decay_rates: float32 [128], P('tp'), as said below
- state_inputs: bfloat16 [8192, 128], P('seq'), may hold values from -6 to 6
- state_readout: bfloat16 [8192, 128], P('seq'), may hold values from -0.5 to 0.5
- skip_gain: float32 [128], P('tp'), may hold values from 0.5 to 1.5
- mixed_inputs: bfloat16 [1536, 8192], P('seq', 'tp'), may hold values from -6 to 6
- out_weight: bfloat16 [8192, 8192], P('tp', 'seq'), may hold values from -0.0625 to 0.0625
Outputs:
- ssm_output: bfloat16 [8192, 8192], P('seq', 'tp')
- projected: bfloat16 [1536, 8192], P('seq', 'tp')
Inputs may be any that keep to these rules, and one draw needn't show every extreme that they name: `step_sizes`: all entries are positive. `decay_rates`: all entries are positive.
All inputs are finite; a program needn't handle non-finite values.
Results may differ from a plain program's by a relative error of at most 0.017.
Values may be sent and summed in bfloat16 or wider, within the bound.
A program may use at most 192 MiB of HBM per device.

v0:
```python
import jax
import jax.numpy as jnp
from jax import lax
from jax.sharding import PartitionSpec as P

HEAD_DIM = 64
STATE = 128
SPAN = 256


def carried_in(array, axis, join, neutral):
    place = lax.axis_index(axis)
    gathered = jax.tree.map(
        lambda a, kind: lax.all_gather(a.astype(kind), axis), array, (jnp.bfloat16, jnp.bfloat16)
    )
    state = jax.tree.map(lambda a, e: jnp.zeros_like(a) + jnp.asarray(e, a.dtype), array, neutral)

    def one(lap, state):
        return join(
            state,
            jax.tree.map(
                lambda a, own: lax.dynamic_index_in_dim(a, lap, 0, False).astype(own.dtype),
                gathered,
                array,
            ),
        )

    return lax.fori_loop(0, place, one, state)


def combine(earlier, latter):
    return (earlier[0] * latter[0], latter[0][:, None, None] * earlier[1] + latter[1])


def per_device(
    ssm_inputs,
    step_sizes,
    decay_rates,
    state_inputs,
    state_readout,
    skip_gain,
    mixed_inputs,
    out_weight,
):
    row_count = ssm_inputs.shape[0]
    head_count = step_sizes.shape[1]
    block_count = row_count // SPAN
    x_blocks = ssm_inputs.reshape(block_count, SPAN, head_count, HEAD_DIM)
    dt_blocks = step_sizes.reshape(block_count, SPAN, head_count)
    b_blocks = state_inputs.reshape(block_count, SPAN, STATE)
    c_blocks = state_readout.reshape(block_count, SPAN, STATE)
    log_decay = jnp.cumsum(-decay_rates[None, None, :] * dt_blocks, axis=1)
    block_decay = log_decay[:, -1, :]
    tail_weight = jnp.exp(block_decay[:, None, :] - log_decay) * dt_blocks
    weighted = (tail_weight[..., None] * x_blocks).astype(jnp.bfloat16)
    block_states = jnp.einsum(
        "cshp,csn->chpn", weighted, b_blocks, preferred_element_type=jnp.float32
    )
    carried = jnp.zeros((head_count, HEAD_DIM, STATE), jnp.float32)
    entering = []
    for block_id in range(block_count):
        entering.append(carried)
        carried = jnp.exp(block_decay[block_id])[:, None, None] * carried + block_states[block_id]
    total_decay = jnp.exp(jnp.sum(block_decay, axis=0))
    identity = (jnp.ones_like(total_decay), jnp.zeros_like(carried))
    decay_before, state_before = carried_in((total_decay, carried), "seq", combine, identity)
    prior_decay = jnp.exp(jnp.cumsum(block_decay, axis=0) - block_decay)
    entering_all = jnp.stack(entering) + prior_decay[:, :, None, None] * state_before[None]
    entering_rounded = entering_all.astype(jnp.bfloat16)
    readout = jnp.einsum(
        "ctn,chpn->cthp", c_blocks, entering_rounded, preferred_element_type=jnp.float32
    )
    y_off = jnp.exp(log_decay)[..., None] * readout
    gram = jnp.einsum("ctn,csn->cts", c_blocks, b_blocks, preferred_element_type=jnp.float32)
    per_head = jnp.transpose(log_decay, (0, 2, 1))
    differ = per_head[:, :, :, None] - per_head[:, :, None, :]
    lower = jnp.tril(jnp.ones((SPAN, SPAN), dtype=bool))
    decay = jnp.exp(jnp.where(lower[None, None], differ, -jnp.inf))
    dt_heads = jnp.transpose(dt_blocks, (0, 2, 1))
    scores = (gram[:, None] * decay * dt_heads[:, :, None, :]).astype(jnp.bfloat16)
    y_diag = jnp.einsum("chts,cshp->cthp", scores, x_blocks, preferred_element_type=jnp.float32)
    combined = y_diag + y_off + skip_gain[None, None, :, None] * x_blocks
    ssm_output = combined.astype(jnp.bfloat16).reshape(row_count, head_count * HEAD_DIM)
    spread_rows = jnp.dot(
        lax.all_gather(mixed_inputs, "seq", axis=0, tiled=True),
        out_weight,
        preferred_element_type=jnp.float32,
    )
    regrouped = lax.all_to_all(
        spread_rows.astype(jnp.bfloat16), "seq", split_axis=0, concat_axis=1, tiled=True
    )
    group_terms = regrouped.astype(jnp.float32)
    projected = lax.psum_scatter(
        group_terms.astype(jnp.bfloat16), "tp", scatter_dimension=1, tiled=True
    )
    return (ssm_output, projected)


def solution(mesh):
    in_specs = (
        P("seq", "tp"),
        P("seq", "tp"),
        P("tp"),
        P("seq", None),
        P("seq", None),
        P("tp"),
        P("seq", "tp"),
        P("tp", "seq"),
    )
    out_specs = (P("seq", "tp"), P("seq", "tp"))
    return jax.shard_map(
        per_device, mesh=mesh, in_specs=in_specs, out_specs=out_specs, check_vma=False
    )
```

profile of v0, /device:TPU:28, one launch (start us, length us, event | category | flops | bytes accessed | tf_op | source)
XLA Modules:
  0.0 322.4 jit_solution(16475436109490359027)
XLA Ops:
  7.2 0.7 all-gather.6.cloned.1.call-update
  8.0 1.0 reshape.138
  8.9 0.7 neg.4
  9.8 2.3 reduce-window.6
  12.3 0.1 copy.63
  12.4 12.9 %reshape.155 = bf16[4,256,32,64]{3,2,1,0:T(8,128)(2,1)} reshape(bf16[1024,2048]{1,0:T(8,128)(2,1)} %param.10) | data formatting | bytes 8388608 | tf_op jit(solution)/shard_map/reshape | solution.py:48
  25.3 10.4 %copy.68 = bf16[4,256,32,64]{1,3,2,0:T(8,128)(2,1)} copy(bf16[4,256,32,64]{3,2,1,0:T(8,128)(2,1)} %reshape.155) | data formatting | bytes 8388608 | tf_op jit(solution)/shard_map/reshape | solution.py:48
  35.9 0.2 fusion.20
  36.1 0.2 slice_reduce_fusion
  36.3 0.1 bitcast_multiply_fusion.1
  36.5 3.5 %fusion.11 = f32[4,32,64,128]{3,2,1,0:T(8,128)S(1)} fusion(bf16[4,256,128,1]{2,1,3,0:T(8,128)(2,1)S(1)} %bitcast.77, bf16[4,256,32,64]{1,3,2,0:T(8,128)(2,1)} %copy.68, f32[4,256,32]{1,2,0:T(8,128)S(1)} %get-tuple-element.75), kind=kOutput, calls=%fused_computation.17 | convolution fusion | flops 543162368 | bytes 8781824 | tf_op jit(solution)/shard_map/cshp,csn->chpn/dot_general | solution.py:56
  40.0 1.5 fusion.19
  41.5 65.5 %all-gather.6.cloned.1.call-done = bf16[1536,2048]{1,0:T(8,128)(2,1)} async-done(((bf16[192,2048]{1,0:T(8,128)(2,1)}), bf16[1536,2048]{1,0:T(8,128)(2,1)}) %all-gather.6.cloned.1.call-update) | async-done | bytes 6291472 | tf_op jit(solution)/shard_map/all_gather | solution.py:85
  107.0 10.0 %convolution_convert_fusion = bf16[1536,1024]{1,0:T(8,128)(2,1)S(1)} fusion(bf16[1536,2048]{1,0:T(8,128)(2,1)} %all-gather.6.cloned.1.call-done, bf16[2048,1024]{1,0:T(8,128)(2,1)} %param.17), kind=kOutput, calls=%fused_computation.21 | convolution fusion | flops 6444023808 | bytes 13631488 | tf_op jit(solution)/shard_map/dot_general | solution.py:84
  117.0 121.2 %all_to_all.19 = bf16[8,192,1024]{2,1,0:T(8,128)(2,1)S(1)} all-to-all(bf16[8,192,1024]{2,1,0:T(8,128)(2,1)S(1)} %bitcast.76), channel_id=1, replica_groups=mesh['seq'=8,'tp'=4] {'seq'}, dimensions={0} | all-to-all | bytes 6291456 | tf_op jit(solution)/shard_map/all_to_all | solution.py:89
  238.2 2.1 copy.84
  240.4 0.6 dynamic-slice
  241.6 0.2 dynamic-update-slice
  241.8 16.9 %all-reduce = bf16[256]{0:T(256)(128)(2,1)S(1)} all-reduce(bf16[256]{0:T(256)(128)(2,1)S(1)} %dynamic-update-slice), channel_id=2, replica_groups=mesh['seq'=8,'tp'=4] {'seq'}, use_global_device_ids=true, to_apply=%add | all-reduce | flops 256 | bytes 1024
  258.9 0.3 fusion.30
  259.2 12.6 %fusion = f32[4,32,256,64]{2,3,1,0:T(8,128)} fusion(bf16[4,256,32,64]{1,3,2,0:T(8,128)(2,1)} %copy.68, f32[4,32,256]{2,1,0:T(8,128)S(1)} %copy.66, f32[4,32,256]{2,1,0:T(8,128)S(1)} %get-tuple-element.78, f32[4,256,256]{2,1,0:T(8,128)S(1)} %fusion.30, pred[256,256]{1,0:T(8,128)(4,1)S(1)} %iota_compare_fusion), kind=kOutput, calls=%fused_computation.3 | convolution fusion | flops 1115684864 | bytes 13959168 | tf_op jit(solution)/shard_map/chts,cshp->cthp/dot_general | solution.py:81
  271.9 9.7 %while.12 = (s32[]{:T(128)}, f32[32,64,128]{2,1,0:T(8,128)S(1)}, s32[]{:T(128)}, bf16[8,32]{1,0:T(8,128)(2,1)S(1)}, bf16[8,32,64,128]{3,2,1,0:T(8,128)(2,1)}, /*index=5*/s32[]{:T(128)}, s32[]{:T(128)}, s32[]{:T(128)}) while((s32[]{:T(128)}, f32[32,64,128]{2,1,0:T(8,128)S(1)}, s32[]{:T(128)}, bf16[8,32]{1,0:T(8,128)(2,1)S(1)}, ...), condition=%wide.region_5.6_spmd, body=%wide.region_4.5_spmd.sunk | while | flops 786469 | bytes 2621887 | solution.py:28
  272.0 1.3 convert_add_fusion.2
  273.3 1.3 convert_add_fusion.2
  274.7 1.3 convert_add_fusion.2
  276.0 1.3 convert_add_fusion.2
  277.4 1.3 convert_add_fusion.2
  278.7 1.3 convert_add_fusion.2
  280.1 1.3 convert_add_fusion.2
  281.6 9.0 %fusion.9 = bf16[4,256,32,64]{1,3,2,0:T(8,128)(2,1)} fusion(bf16[4,256,32,64]{1,3,2,0:T(8,128)(2,1)} %copy.68, f32[4,32,256,64]{2,3,1,0:T(8,128)} %fusion, f32[32]{0:T(128)S(1)} %copy-done.3, f32[4,256,32]{1,2,0:T(8,128)S(1)} %get-tuple-element.76, bf16[4,256,128,1]{2,1,3,0:T(8,128)(2,1)S(1)} %bitcast.73, f32[1,32,64,128]{3,2,1,0:T(8,128)S(1)} %get-tuple-element.72, ...), kind=kOutput, calls=%fused_computation.14 | convolution fusion | flops 555745280 | bytes 21365392 | tf_op jit(solution)/shard_map/ctn,chpn->cthp/dot_general | solution.py:70
  290.7 12.9 %copy.78 = bf16[4,256,32,64]{3,2,1,0:T(8,128)(2,1)} copy(bf16[4,256,32,64]{1,3,2,0:T(8,128)(2,1)} %fusion.9) | data formatting | bytes 8388608
  303.6 12.3 %reshape.154 = bf16[1024,2048]{1,0:T(8,128)(2,1)} reshape(bf16[4,256,32,64]{3,2,1,0:T(8,128)(2,1)} %copy.78) | data formatting | bytes 8388608
  (41 shorter events, 1.0 us)
Async XLA Ops:
  7.2 251.7 %copy-start = (bf16[1024,128]{1,0:T(8,128)(2,1)S(1)}, bf16[1024,128]{1,0:T(8,128)(2,1)}, u32[]{:S(2)}) copy-start(bf16[1024,128]{1,0:T(8,128)(2,1)} %param.14) | copy-start | bytes 786436
  7.2 99.8 %all-gather.6.cloned.1.call-start = ((), (), s32[]{:S(2)}) async-start(), calls=%async_computation.3 | async-start | bytes 7077888 | tf_op jit(solution)/shard_map/all_gather | solution.py:85
  7.9 263.9 %all-gather.4.cloned.1.call-start = ((), (), s32[]{:S(2)}) async-start(), calls=%async_computation.2 | async-start | bytes 4718592 | tf_op jit(solution)/shard_map/all_gather | solution.py:14
  25.3 11.0 %copy-start.2 = (f32[1024,32]{0,1:T(8,128)S(1)}, f32[1024,32]{0,1:T(8,128)}, u32[]{:S(2)}) copy-start(f32[1024,32]{0,1:T(8,128)} %param.11) | copy-start | bytes 393220
  25.3 11.1 %copy-start.1 = (bf16[1024,128]{1,0:T(8,128)(2,1)S(1)}, bf16[1024,128]{1,0:T(8,128)(2,1)}, u32[]{:S(2)}) copy-start(bf16[1024,128]{1,0:T(8,128)(2,1)} %param.13) | copy-start | bytes 786436
  41.5 274.4 %reduce-scatter.2.cloned.1.call-start = ((), (), s32[]{:S(2)}) async-start(), calls=%async_computation.4 | async-start | bytes 3932160 | tf_op jit(solution)/shard_map/reduce_scatter | solution.py:93
  238.2 2.2 copy-start.4
  271.9 9.7 %copy-start.3 = (f32[32]{0:T(128)S(1)}, f32[32]{0:T(128)}, u32[]{:S(2)}) copy-start(f32[32]{0:T(128)} %param.15) | copy-start | bytes 388
Sparse Core Ops, SparseCore 0:
  10.2 96.8 all-gather.5
  109.1 121.5 all-gather.3
  240.5 38.6 reduce-scatter.1
where the time goes:
time: 324 us; the launch traced here: 322 us
  blocking collectives  138 us (43%)
  waiting for transfers between devices  66.2 us (20%)
  local copies, waits for them, and re-layouts  53.1 us (16%)
  matrix products  35.4 us (11%)
  other arithmetic  14.5 us (4%)
  between operations  14.5 us (4%)
    all_to_all x1, blocking collectives, per_device(): lax.all_to_all(spread_rows.astype(jnp.bfloat16), 'seq', split_axis=0, con...  121 us
    all_gather x1, waiting for transfers between devices, per_device(): lax.all_gather(mixed_inputs, 'seq', axis=0, tiled=True)  65.5 us
    unnamed x15, local copies, waits for them, and re-layouts  26.1 us
    reshape x2, local copies, waits for them, and re-layouts, per_device(): x_blocks = ssm_inputs.reshape(block_count, SPAN, head_count, HEAD_DIM)  23.4 us
    unnamed x1, blocking collectives  16.9 us
    dot_general x1, matrix products, per_device(): jnp.einsum('chts,cshp->cthp', scores, x_blocks, preferred_element_type=jn...  12.6 us
    dot_general x1, matrix products, per_device(): jnp.dot(lax.all_gather(mixed_inputs, 'seq', axis=0, tiled=True), out_weig...  10 us
    add x7, other arithmetic, combine(): latter[0][:, None, None] * earlier[1] + latter[1]  9.14 us
  transfers between devices with their start and end apart: 3, of which 1 were waited for; matrix products, arithmetic and copies ran while one was open for 32% of the time, Pallas kernels for 0%

commit v1 on v0

v1 whole, which is shorter than its diff:
```python
import functools

import jax
import jax.numpy as jnp
from jax import lax
from jax.experimental import pallas as pl
from jax.experimental.pallas import tpu as pltpu
from jax.sharding import PartitionSpec as P

HEAD_DIM = 64
STATE = 128
SPAN = 256
PAIR = 2 * HEAD_DIM
GROUP = 8
MESH = pl.DeviceIdType.MESH
F32 = jnp.float32
BF16 = jnp.bfloat16
HIGH = lax.Precision.HIGHEST


def dot(a, b, **kw):
    return jnp.dot(a, b, preferred_element_type=F32, **kw)


def pair_lanes(first, second, rows):
    lane = lax.broadcasted_iota(jnp.int32, (rows, PAIR), 1)
    return jnp.where(
        lane < HEAD_DIM,
        jnp.broadcast_to(first, (rows, PAIR)),
        jnp.broadcast_to(second, (rows, PAIR)),
    )


def states_kernel(
    x_ref, dt_ref, dtt_ref, rate_ref, ratec_ref, bt_ref,
    block_ref, ld_ref, ldt_ref, dec_ref, tot_ref, totdec_ref,
    carry, carry_dec,
):
    block_id = pl.program_id(0)
    heads = dt_ref.shape[1]
    row = lax.broadcasted_iota(jnp.int32, (SPAN, SPAN), 0)
    col = lax.broadcasted_iota(jnp.int32, (SPAN, SPAN), 1)
    lower = (row >= col).astype(F32)
    upper = (row <= col).astype(F32)
    dt = dt_ref[...]
    ld = dot(lower, -rate_ref[...] * dt, precision=HIGH)
    ldt_ref[...] = dot(-ratec_ref[...] * dtt_ref[...], upper, precision=HIGH)
    for g in range(heads // GROUP):
        ld_ref[g] = ld[:, g * GROUP:(g + 1) * GROUP]
    last = ld[SPAN - 1:SPAN, :]
    tail = jnp.exp(last - ld) * dt
    last_dec = jnp.exp(last)

    @pl.when(block_id == 0)
    def _():
        carry[...] = jnp.zeros_like(carry)
        carry_dec[...] = jnp.ones_like(carry_dec)

    bt = bt_ref[...]
    for j in range(heads // 2):
        cols = slice(j * PAIR, (j + 1) * PAIR)
        weight = pair_lanes(tail[:, 2 * j:2 * j + 1], tail[:, 2 * j + 1:2 * j + 2], SPAN)
        weighted = (weight * x_ref[:, cols].astype(F32)).astype(BF16)
        state = dot(bt, weighted)
        block_ref[0, :, cols] = state
        dec = pair_lanes(last_dec[:, 2 * j:2 * j + 1], last_dec[:, 2 * j + 1:2 * j + 2], 8)
        dec_ref[0, :, cols] = dec
        carry[:, cols] = dec[0:1] * carry[:, cols] + state
        carry_dec[:, cols] = dec * carry_dec[:, cols]
    tot_ref[...] = carry[...].astype(BF16)
    totdec_ref[...] = carry_dec[...]


def local_states(x, dt, dtt, rates, bt):
    rows, width = x.shape
    heads = dt.shape[1]
    blocks = rows // SPAN
    groups = heads // GROUP
    return pl.pallas_call(
        states_kernel,
        grid=(blocks,),
        in_specs=[
            pl.BlockSpec((SPAN, width), lambda b: (b, 0)),
            pl.BlockSpec((SPAN, heads), lambda b: (b, 0)),
            pl.BlockSpec((heads, SPAN), lambda b: (0, b)),
            pl.BlockSpec((1, heads), lambda b: (0, 0)),
            pl.BlockSpec((heads, 1), lambda b: (0, 0)),
            pl.BlockSpec((STATE, SPAN), lambda b: (0, b)),
        ],
        out_specs=[
            pl.BlockSpec((1, STATE, width), lambda b: (b, 0, 0)),
            pl.BlockSpec((groups, SPAN, GROUP), lambda b: (0, b, 0)),
            pl.BlockSpec((heads, SPAN), lambda b: (0, b)),
            pl.BlockSpec((1, 8, width), lambda b: (b, 0, 0)),
            pl.BlockSpec((STATE, width), lambda b: (0, 0)),
            pl.BlockSpec((8, width), lambda b: (0, 0)),
        ],
        out_shape=[
            jax.ShapeDtypeStruct((blocks, STATE, width), F32),
            jax.ShapeDtypeStruct((groups, rows, GROUP), F32),
            jax.ShapeDtypeStruct((heads, rows), F32),
            jax.ShapeDtypeStruct((blocks, 8, width), F32),
            jax.ShapeDtypeStruct((STATE, width), BF16),
            jax.ShapeDtypeStruct((8, width), F32),
        ],
        scratch_shapes=[pltpu.VMEM((STATE, width), F32), pltpu.VMEM((8, width), F32)],
        compiler_params=pltpu.CompilerParams(dimension_semantics=("arbitrary",)),
        name="states",
    )(x, dt, dtt, rates[None, :], rates[:, None], bt)


def output_kernel(
    x_ref, dtt_ref, ld_ref, ldt_ref, bt_ref, c_ref, block_ref, dec_ref, before_ref, skip_ref,
    out_ref, carry,
):
    block_id = pl.program_id(0)
    g = pl.program_id(1)
    half = SPAN // 2

    @pl.when(block_id == 0)
    def _():
        carry[g] = before_ref[...]

    entering = carry[g]
    c = c_ref[...]
    readout = dot(c, entering.astype(BF16))
    carry[g] = dec_ref[0, 0:1] * entering + block_ref[0]
    gram = dot(c, bt_ref[...])
    row = lax.broadcasted_iota(jnp.int32, (half, half), 0)
    col = lax.broadcasted_iota(jnp.int32, (half, half), 1)
    lower = row >= col
    gram_top = jnp.where(lower, gram[:half, :half], 0.0)
    gram_low = jnp.where(lower, gram[half:, half:], 0.0)
    gram_off = gram[half:, :half]
    ld = ld_ref[0]
    grow = jnp.exp(ld)
    for j in range(GROUP // 2):
        cols = slice(j * PAIR, (j + 1) * PAIR)
        x = x_ref[:, cols]
        tops, lows = [], []
        for h in (2 * j, 2 * j + 1):
            across = jnp.broadcast_to(ld[:, h:h + 1], (SPAN, half))
            left, right = ldt_ref[h:h + 1, :half], ldt_ref[h:h + 1, half:]
            dt_left, dt_right = dtt_ref[h:h + 1, :half], dtt_ref[h:h + 1, half:]
            top = gram_top * jnp.exp(jnp.minimum(across[:half] - left, 0.0)) * dt_left
            off = gram_off * jnp.exp(jnp.minimum(across[half:] - left, 0.0)) * dt_left
            low = gram_low * jnp.exp(jnp.minimum(across[half:] - right, 0.0)) * dt_right
            tops.append(dot(top.astype(BF16), x[:half]))
            lows.append(
                dot(jnp.concatenate([off.astype(BF16), low.astype(BF16)], axis=1), x)
            )
        lane = lax.broadcasted_iota(jnp.int32, (half, PAIR), 1)
        mine = lane < HEAD_DIM
        scale = pair_lanes(grow[:, 2 * j:2 * j + 1], grow[:, 2 * j + 1:2 * j + 2], SPAN)
        rest = scale * readout[:, cols] + skip_ref[:, cols] * x.astype(F32)
        out_ref[:half, cols] = (jnp.where(mine, tops[0], tops[1]) + rest[:half]).astype(BF16)
        out_ref[half:, cols] = (jnp.where(mine, lows[0], lows[1]) + rest[half:]).astype(BF16)


def scan_output(x, dtt, ld, ldt, bt, c, block_states, dec, before, skip):
    rows, width = x.shape
    blocks = rows // SPAN
    groups = ld.shape[0]
    wide = width // groups
    return pl.pallas_call(
        output_kernel,
        grid=(blocks, groups),
        in_specs=[
            pl.BlockSpec((SPAN, wide), lambda b, g: (b, g)),
            pl.BlockSpec((GROUP, SPAN), lambda b, g: (g, b)),
            pl.BlockSpec((1, SPAN, GROUP), lambda b, g: (g, b, 0)),
            pl.BlockSpec((GROUP, SPAN), lambda b, g: (g, b)),
            pl.BlockSpec((STATE, SPAN), lambda b, g: (0, b)),
            pl.BlockSpec((SPAN, STATE), lambda b, g: (b, 0)),
            pl.BlockSpec((1, STATE, wide), lambda b, g: (b, 0, g)),
            pl.BlockSpec((1, 8, wide), lambda b, g: (b, 0, g)),
            pl.BlockSpec((STATE, wide), lambda b, g: (0, g)),
            pl.BlockSpec((1, wide), lambda b, g: (0, g)),
        ],
        out_specs=pl.BlockSpec((SPAN, wide), lambda b, g: (b, g)),
        out_shape=jax.ShapeDtypeStruct((rows, width), BF16),
        scratch_shapes=[pltpu.VMEM((groups, STATE, wide), F32)],
        compiler_params=pltpu.CompilerParams(dimension_semantics=("arbitrary", "arbitrary")),
        name="scan_output",
    )(x, dtt, ld, ldt, bt, c, block_states, dec, before, skip)


def exchange_kernel(
    n, tps,
    tot_ref, totdec_ref, mixed_ref, weight_ref,
    proj_ref, before_ref,
    cw, ccw, part, red, fin, landed,
    st_out, st_in, dec_out, dec_in, total, total_dec, before_dec,
    ring_send, ring_recv, red_send, red_recv, fin_send, fin_recv, st_send, st_recv,
):
    s = lax.axis_index("seq")
    t = lax.axis_index("tp")
    odd = s % 2
    place = (1 - odd) * (s // 2) + odd * (n - 1 - s // 2)

    def member(at):
        at = (at + 2 * n) % n
        back = at // (n // 2)
        return (1 - back) * (2 * at) + back * (2 * (n - 1 - at) + 1)

    right, left = member(place + 1), member(place - 1)
    rows = mixed_ref.shape[0]
    half = rows // 2
    quarter = rows // tps
    width = weight_ref.shape[1]
    steps = n // 2
    per = n // tps
    rounds = n.bit_length() - 1

    def remote(src, dst, send, recv, where):
        return pltpu.make_async_remote_copy(
            src_ref=src, dst_ref=dst, send_sem=send, recv_sem=recv,
            device_id=where, device_id_type=MESH,
        )

    def hop(way, k, h):
        slots = (cw, ccw)[way]
        span = pl.ds(h * half, half)
        src = mixed_ref.at[span] if k == 0 else slots.at[k - 1, span]
        dst = cw.at[k, span] if k == steps - 1 else slots.at[k, span]
        return remote(
            src, dst, ring_send.at[way, k, h], ring_recv.at[way, k, h],
            {"seq": (right, left)[way]},
        )

    def carries(way, k, h):
        return k < steps and (k < steps - 1 or h == way)

    def passing(r):
        bit = (s // 2 ** r) % 2
        partner = s + (1 - 2 * bit) * 2 ** r
        src = tot_ref if r == 0 else st_out.at[r - 1]
        dec = totdec_ref if r == 0 else dec_out.at[r - 1]
        return bit, (
            remote(src, st_in.at[r], st_send.at[r, 0], st_recv.at[r, 0], {"seq": partner}),
            remote(dec, dec_in.at[r], st_send.at[r, 1], st_recv.at[r, 1], {"seq": partner}),
        )

    def start_round(r):
        bit, copies = passing(r)
        if r < rounds - 1:
            for copy in copies:
                copy.start()
        else:
            @pl.when(bit == 0)
            def _():
                for copy in copies:
                    copy.start()

    def finish_round(r):
        bit, copies = passing(r)

        def lands():
            for copy in copies:
                copy.wait_recv()

        @pl.when(bit == 1)
        def _():
            lands()

            @pl.loop(0, total.shape[1] // 256)
            def _(i):
                cols = pl.ds(pl.multiple_of(i * 256, 256), 256)
                other = st_in[r, :, cols].astype(F32)
                before_ref[:, cols] += before_dec[0:1, cols] * other
                if r < rounds - 1:
                    fresh = total_dec[0:1, cols] * other + total[:, cols]
                    total[:, cols] = fresh
                    st_out[r, :, cols] = fresh.astype(BF16)

            before_dec[...] *= dec_in[r]
            if r < rounds - 1:
                total_dec[...] *= dec_in[r]
                dec_out[r] = total_dec[...]

        if r < rounds - 1:
            @pl.when(bit == 0)
            def _():
                lands()

                @pl.loop(0, total.shape[1] // 256)
                def _(i):
                    cols = pl.ds(pl.multiple_of(i * 256, 256), 256)
                    other = st_in[r, :, cols].astype(F32)
                    fresh = dec_in[r, 0:1, cols] * total[:, cols] + other
                    total[:, cols] = fresh
                    st_out[r, :, cols] = fresh.astype(BF16)

                total_dec[...] *= dec_in[r]
                dec_out[r] = total_dec[...]

            start_round(r + 1)

    def multiply(u, block):
        tile = min(256, width)

        @pl.loop(0, width // tile)
        def _(i):
            cols = pl.ds(pl.multiple_of(i * tile, tile), tile)
            value = dot(block[...], weight_ref[:, cols]).astype(BF16)
            for q in range(tps):
                part[u, q, :, cols] = value[q * quarter:(q + 1) * quarter]

    def reduction(u, j):
        peer = (t + j) % tps
        return remote(
            part.at[u, peer], red.at[u, j - 1], red_send.at[u, j - 1], red_recv.at[u, j - 1],
            {"tp": peer},
        )

    def begin(u, block):
        multiply(u, block)
        for j in range(1, tps):
            reduction(u, j).start()

    def delivery(u, owner):
        return remote(
            fin.at[u], landed.at[s % per, t], fin_send.at[u], fin_recv.at[s % per, t],
            {"seq": owner, "tp": s // per},
        )

    def close(u, owner):
        for j in range(1, tps):
            reduction(u, j).wait_recv()
        value = part[u, t].astype(F32)
        for j in range(1, tps):
            value = value + red[u, j - 1].astype(F32)
        fin[u] = value.astype(BF16)
        if u:
            delivery(u, owner).start()
        else:
            @pl.when(t == s // per)
            def _():
                pltpu.make_async_copy(
                    fin.at[u], landed.at[s % per, t], fin_recv.at[s % per, t]
                ).start()

            @pl.when(t != s // per)
            def _():
                delivery(u, owner).start()

    start_round(0)
    for h in range(2):
        for way in range(2):
            if carries(way, 0, h):
                hop(way, 0, h).start()
    total[...] = tot_ref[...].astype(F32)
    total_dec[...] = totdec_ref[...]
    before_ref[...] = jnp.zeros_like(before_ref)
    before_dec[...] = jnp.ones_like(before_dec)

    begin(0, mixed_ref)
    waiting = [(0, s)]
    done = []
    for k in range(steps):
        if k < rounds:
            finish_round(k)
        for h in range(2):
            for way in range(2):
                if carries(way, k, h):
                    hop(way, k, h).wait_recv()
                    if carries(way, k + 1, h):
                        hop(way, k + 1, h).start()
        fresh = [(1 + 2 * k, member(place - 1 - k))]
        begin(1 + 2 * k, cw.at[k])
        if k < steps - 1:
            begin(2 + 2 * k, ccw.at[k])
            fresh.append((2 + 2 * k, member(place + 1 + k)))
        for u, owner in waiting:
            close(u, owner)
        done += waiting
        waiting = fresh
    for r in range(min(steps, rounds), rounds):
        finish_round(r)
    for u, owner in waiting:
        close(u, owner)
    done += waiting

    for g in range(per):
        for q in range(tps):
            remote(
                fin.at[0], landed.at[g, q], fin_send.at[0], fin_recv.at[g, q], {"seq": right}
            ).wait_recv()
            proj_ref[q * quarter:(q + 1) * quarter, g * width:(g + 1) * width] = landed[g, q]

    for k in range(steps):
        for h in range(2):
            for way in range(2):
                if carries(way, k, h):
                    hop(way, k, h).wait_send()
    for u, owner in done:
        for j in range(1, tps):
            reduction(u, j).wait_send()
        if u:
            delivery(u, owner).wait_send()
        else:
            @pl.when(t != s // per)
            def _():
                delivery(u, owner).wait_send()
    for r in range(rounds):
        bit, copies = passing(r)
        if r < rounds - 1:
            for copy in copies:
                copy.wait_send()
        else:
            @pl.when(bit == 0)
            def _():
                for copy in copies:
                    copy.wait_send()


def exchange(n, tps, tot, totdec, mixed, weight):
    rows, depth = mixed.shape
    width = weight.shape[1]
    quarter = rows // tps
    steps = n // 2
    per = n // tps
    rounds = n.bit_length() - 1
    state = tot.shape
    dec = totdec.shape
    dma = pltpu.SemaphoreType.DMA
    vmem = pl.BlockSpec(memory_space=pltpu.VMEM)
    return pl.pallas_call(
        functools.partial(exchange_kernel, n, tps),
        in_specs=[vmem] * 4,
        out_specs=[vmem] * 2,
        out_shape=[
            jax.ShapeDtypeStruct((rows, per * width), BF16),
            jax.ShapeDtypeStruct(state, F32),
        ],
        scratch_shapes=[
            pltpu.VMEM((steps, rows, depth), BF16),
            pltpu.VMEM((max(steps - 1, 1), rows, depth), BF16),
            pltpu.VMEM((n, tps, quarter, width), BF16),
            pltpu.VMEM((n, tps - 1, quarter, width), BF16),
            pltpu.VMEM((n, quarter, width), BF16),
            pltpu.VMEM((per, tps, quarter, width), BF16),
            pltpu.VMEM((rounds - 1,) + state, BF16),
            pltpu.VMEM((rounds,) + state, BF16),
            pltpu.VMEM((rounds - 1,) + dec, F32),
            pltpu.VMEM((rounds,) + dec, F32),
            pltpu.VMEM(state, F32),
            pltpu.VMEM(dec, F32),
            pltpu.VMEM(dec, F32),
            dma((2, steps, 2)),
            dma((2, steps, 2)),
            dma((n, tps - 1)),
            dma((n, tps - 1)),
            dma((n,)),
            dma((per, tps)),
            dma((rounds, 2)),
            dma((rounds, 2)),
        ],
        compiler_params=pltpu.CompilerParams(
            has_side_effects=True, vmem_limit_bytes=60 * 2 ** 20
        ),
        name="exchange",
    )(tot, totdec, mixed, weight)


def per_device(
    n, tps,
    ssm_inputs,
    step_sizes,
    decay_rates,
    state_inputs,
    state_readout,
    skip_gain,
    mixed_inputs,
    out_weight,
):
    dtt = step_sizes.T
    bt = state_inputs.T
    skip = jnp.repeat(skip_gain, HEAD_DIM)[None, :]
    block_states, ld, ldt, dec, tot, totdec = local_states(
        ssm_inputs, step_sizes, dtt, decay_rates, bt
    )
    projected, before = exchange(n, tps, tot, totdec, mixed_inputs, out_weight)
    ssm_output = scan_output(
        ssm_inputs, dtt, ld, ldt, bt, state_readout, block_states, dec, before, skip
    )
    return (ssm_output, projected)


def solution(mesh):
    in_specs = (
        P("seq", "tp"),
        P("seq", "tp"),
        P("tp"),
        P("seq", None),
        P("seq", None),
        P("tp"),
        P("seq", "tp"),
        P("tp", "seq"),
    )
    out_specs = (P("seq", "tp"), P("seq", "tp"))
    return jax.shard_map(
        functools.partial(per_device, mesh.shape["seq"], mesh.shape["tp"]),
        mesh=mesh, in_specs=in_specs, out_specs=out_specs, check_vma=False,
    )
```

time: 324 us -> 160 us (0.49)
  the two profiles are of different devices: /device:TPU:28 before, /device:TPU:3 now
where the time goes in v1:
time: 160 us; the launch traced here: 159 us
  Pallas kernels  151 us (94%)
  local copies, waits for them, and re-layouts  7.34 us (5%)
    pallas_call x1, Pallas kernels, exchange(): pl.pallas_call(functools.partial(exchange_kernel, n, tps), in_specs=[vmem...  120 us
    pallas_call x1, Pallas kernels, scan_output(): pl.pallas_call(output_kernel, grid=(blocks, groups), in_specs=[pl.BlockSp...  19 us
    pallas_call x1, Pallas kernels, local_states(): pl.pallas_call(states_kernel, grid=(blocks,), in_specs=[pl.BlockSpec((SPA...  11.9 us
    unnamed x5, local copies, waits for them, and re-layouts  4.61 us

profile of v1, /device:TPU:3, one launch (start us, length us, event | category | flops | bytes accessed | tf_op | source)
XLA Modules:
  0.0 159.1 jit_solution(620829234628781701)
XLA Ops:
  0.6 0.7 broadcast_in_dim.11
  1.4 0.7 broadcast_in_dim_reshape.3.skip_ref
  2.0 1.3 copy.12.ratec_ref
  3.4 1.8 %copy.10 = bf16[1024,128]{0,1:T(8,128)(2,1)} copy(bf16[1024,128]{1,0:T(8,128)(2,1)} %param.11) | data formatting | bytes 524288 | tf_op args[3]
  5.2 1.9 %copy.11.dt_ref = f32[1024,32]{1,0:T(8,128)} copy(f32[1024,32]{0,1:T(8,128)} %param.9) | data formatting | bytes 262144 | tf_op args[1]
  7.1 11.9 %states.1 = (f32[4,128,2048]{2,1,0:T(8,128)}, f32[4,1024,8]{2,1,0:T(8,128)}, f32[32,1024]{1,0:T(8,128)}, f32[4,8,2048]{2,1,0:T(8,128)}, bf16[128,2048]{1,0:T(8,128)(2,1)}, /*index=5*/f32[8,2048]{1,0:T(8,128)}) custom-call(bf16[1024,2048]{1,0:T(8,128)(2,1)} %x_ref.3, f32[1024,32]{1,0:T(8,128)} %copy.11.dt_ref, f32[32,1024]{1,0:T(8,128)} %bitcast.6, ...), custom_call_target="tpu_custom_call" | custom-call | tf_op jit(solution)/shard_map/states/pallas_call | solution.py:79
  19.0 120.2 %exchange.1 = (bf16[192,2048]{1,0:T(8,128)(2,1)}, f32[128,2048]{1,0:T(8,128)}) custom-call(bf16[128,2048]{1,0:T(8,128)(2,1)} %get-tuple-element.14.tot_ref, f32[8,2048]{1,0:T(8,128)} %get-tuple-element.15.totdec_ref, bf16[192,2048]{1,0:T(8,128)(2,1)} %mixed_ref.1, bf16[2048,1024]{1,0:T(8,128)(2,1)} %weight_ref.1), custom_call_target="tpu_custom_call" | custom-call | tf_op jit(solution)/shard_map/exchange/pallas_call | solution.py:428
  139.2 0.0 copy-start
  139.3 19.0 %scan_output.1 = bf16[1024,2048]{1,0:T(8,128)(2,1)} custom-call(bf16[1024,2048]{1,0:T(8,128)(2,1)} %x_ref.3, f32[32,1024]{1,0:T(8,128)} %bitcast.7, f32[4,1024,8]{2,1,0:T(8,128)} %get-tuple-element.10.ld_ref, f32[32,1024]{1,0:T(8,128)} %get-tuple-element.11.ldt_ref, bf16[128,1024]{1,0:T(8,128)(2,1)} %bitcast.5, bf16[1024,128]{1,0:T(8,128)(2,1)} %c_ref.1, ...), custom_call_target="tpu_custom_call" | custom-call | tf_op jit(solution)/shard_map/scan_output/pallas_call | solution.py:165
  158.2 0.0 copy-done
  158.2 0.9 copy.14
Async XLA Ops:
  139.2 19.0 %copy-start = (bf16[192,2048]{1,0:T(8,128)(2,1)S(1)}, bf16[192,2048]{1,0:T(8,128)(2,1)}, u32[]{:S(2)}) copy-start(bf16[192,2048]{1,0:T(8,128)(2,1)} %get-tuple-element.21) | copy-start | bytes 2359300

commit v2 on v1

v2 whole, which is shorter than its diff:
```python
import functools

import jax
import jax.numpy as jnp
from jax import lax
from jax.experimental import pallas as pl
from jax.experimental.pallas import tpu as pltpu
from jax.sharding import PartitionSpec as P

HEAD_DIM = 64
STATE = 128
SPAN = 256
PAIR = 2 * HEAD_DIM
GROUP = 8
MESH = pl.DeviceIdType.MESH
F32 = jnp.float32
BF16 = jnp.bfloat16
HIGH = lax.Precision.HIGHEST


def dot(a, b, **kw):
    return jnp.dot(a, b, preferred_element_type=F32, **kw)


def pair_lanes(first, second, rows):
    lane = lax.broadcasted_iota(jnp.int32, (rows, PAIR), 1)
    return jnp.where(
        lane < HEAD_DIM,
        jnp.broadcast_to(first, (rows, PAIR)),
        jnp.broadcast_to(second, (rows, PAIR)),
    )


def transposed_dot(a, b, **kw):
    return lax.dot_general(a, b, (((0,), (0,)), ((), ())), preferred_element_type=F32, **kw)


def block_prepare(b, x, dt_ref, rate_ref, b_ref, blocks, lds, ldts, dtts, decs, total, total_dec):
    rows = pl.ds(pl.multiple_of(b * SPAN, SPAN), SPAN)
    heads = dt_ref.shape[1]
    row = lax.broadcasted_iota(jnp.int32, (SPAN, SPAN), 0)
    col = lax.broadcasted_iota(jnp.int32, (SPAN, SPAN), 1)
    lower = (row >= col).astype(F32)
    upper = (row <= col).astype(F32)
    same = (row == col).astype(F32)
    dt = dt_ref[rows, :]
    step = -rate_ref[...] * dt
    ld = dot(lower, step, precision=HIGH)
    ldts[b] = transposed_dot(step, upper, precision=HIGH)
    dtts[b] = transposed_dot(dt, same, precision=HIGH)
    for g in range(heads // GROUP):
        lds[b, g] = ld[:, g * GROUP:(g + 1) * GROUP]
    last = ld[SPAN - 1:SPAN, :]
    tail = jnp.exp(last - ld) * dt
    last_dec = jnp.exp(last)
    bt = b_ref[rows, :].astype(F32).T.astype(BF16)
    for j in range(heads // 2):
        cols = slice(j * PAIR, (j + 1) * PAIR)
        weight = pair_lanes(tail[:, 2 * j:2 * j + 1], tail[:, 2 * j + 1:2 * j + 2], SPAN)
        weighted = (weight * x[rows, cols].astype(F32)).astype(BF16)
        state = dot(bt, weighted)
        blocks[b, :, cols] = state
        dec = pair_lanes(last_dec[:, 2 * j:2 * j + 1], last_dec[:, 2 * j + 1:2 * j + 2], 8)
        decs[b, :, cols] = dec
        total[:, cols] = dec[0:1] * total[:, cols] + state
        total_dec[:, cols] = dec * total_dec[:, cols]


def block_inside(b, g, wide, x, b_ref, c_ref, skip_ref, lds, ldts, dtts, diag):
    half = SPAN // 2
    rows = pl.ds(pl.multiple_of(b * SPAN, SPAN), SPAN)
    gram = lax.dot_general(
        c_ref[rows, :], b_ref[rows, :], (((1,), (1,)), ((), ())), preferred_element_type=F32
    )
    row = lax.broadcasted_iota(jnp.int32, (half, half), 0)
    col = lax.broadcasted_iota(jnp.int32, (half, half), 1)
    lower = row >= col
    gram_top = jnp.where(lower, gram[:half, :half], 0.0)
    gram_low = jnp.where(lower, gram[half:, half:], 0.0)
    gram_off = gram[half:, :half]
    ld = lds[b, g]
    heads = pl.ds(pl.multiple_of(g * GROUP, GROUP), GROUP)
    ldt = ldts[b, heads, :]
    dtt = dtts[b, heads, :]
    lane = lax.broadcasted_iota(jnp.int32, (half, PAIR), 1)
    mine = lane < HEAD_DIM
    for j in range(GROUP // 2):
        xs = x[rows, pl.ds(pl.multiple_of(g * wide + j * PAIR, PAIR), PAIR)]
        tops, lows = [], []
        for h in (2 * j, 2 * j + 1):
            across = jnp.broadcast_to(ld[:, h:h + 1], (SPAN, half))
            left, right = ldt[h:h + 1, :half], ldt[h:h + 1, half:]
            dt_left, dt_right = dtt[h:h + 1, :half], dtt[h:h + 1, half:]
            top = gram_top * jnp.exp(jnp.minimum(across[:half] - left, 0.0)) * dt_left
            off = gram_off * jnp.exp(jnp.minimum(across[half:] - left, 0.0)) * dt_left
            low = gram_low * jnp.exp(jnp.minimum(across[half:] - right, 0.0)) * dt_right
            tops.append(dot(top.astype(BF16), xs[:half]))
            lows.append(
                dot(jnp.concatenate([off.astype(BF16), low.astype(BF16)], axis=1), xs)
            )
        skip = skip_ref[:, pl.ds(pl.multiple_of(g * wide + j * PAIR, PAIR), PAIR)]
        rest = skip * xs.astype(F32)
        cols = slice(j * PAIR, (j + 1) * PAIR)
        diag[b, g, :half, cols] = jnp.where(mine, tops[0], tops[1]) + rest[:half]
        diag[b, g, half:, cols] = jnp.where(mine, lows[0], lows[1]) + rest[half:]


def block_finish(b, g, wide, x, c_ref, before, blocks, decs, lds, diag):
    rows = pl.ds(pl.multiple_of(b * SPAN, SPAN), SPAN)
    cols = pl.ds(pl.multiple_of(g * wide, wide), wide)
    entering = before[:, cols]
    readout = dot(c_ref[rows, :], entering.astype(BF16))
    before[:, cols] = decs[b, 0:1, cols] * entering + blocks[b, :, cols]
    grow = jnp.exp(lds[b, g])
    for j in range(GROUP // 2):
        part = slice(j * PAIR, (j + 1) * PAIR)
        scale = pair_lanes(grow[:, 2 * j:2 * j + 1], grow[:, 2 * j + 1:2 * j + 2], SPAN)
        value = diag[b, g, :, part] + scale * readout[:, part]
        x[rows, pl.ds(pl.multiple_of(g * wide + j * PAIR, PAIR), PAIR)] = value.astype(BF16)


def exchange_kernel(
    n, tps,
    x_hbm, dt_ref, rate_ref, b_ref, c_ref, skip_ref, mixed_ref, weight_hbm,
    out_hbm, proj_ref,
    x, weight_ref, blocks, lds, ldts, dtts, decs, diag, before_ref, tot_ref, totdec_ref,
    cw, ccw, part, red, fin, landed,
    st_out, st_in, dec_out, dec_in, total, total_dec, before_dec,
    ring_send, ring_recv, red_send, red_recv, fin_send, fin_recv, st_send, st_recv,
    load, store,
):
    s = lax.axis_index("seq")
    t = lax.axis_index("tp")
    odd = s % 2
    place = (1 - odd) * (s // 2) + odd * (n - 1 - s // 2)

    def member(at):
        at = (at + 2 * n) % n
        back = at // (n // 2)
        return (1 - back) * (2 * at) + back * (2 * (n - 1 - at) + 1)

    right, left = member(place + 1), member(place - 1)
    rows = mixed_ref.shape[0]
    half = rows // 2
    quarter = rows // tps
    width = weight_ref.shape[1]
    steps = n // 2
    per = n // tps
    rounds = n.bit_length() - 1
    block_count, groups = lds.shape[0], lds.shape[1]
    wide = x.shape[1] // groups

    def remote(src, dst, send, recv, where):
        return pltpu.make_async_remote_copy(
            src_ref=src, dst_ref=dst, send_sem=send, recv_sem=recv,
            device_id=where, device_id_type=MESH,
        )

    def hop(way, k, h):
        slots = (cw, ccw)[way]
        span = pl.ds(h * half, half)
        src = mixed_ref.at[span] if k == 0 else slots.at[k - 1, span]
        dst = cw.at[k, span] if k == steps - 1 else slots.at[k, span]
        return remote(
            src, dst, ring_send.at[way, k, h], ring_recv.at[way, k, h],
            {"seq": (right, left)[way]},
        )

    def carries(way, k, h):
        return k < steps and (k < steps - 1 or h == way)

    def combine(r, upper):
        @pl.loop(0, total.shape[1] // 256)
        def _(i):
            cols = pl.ds(pl.multiple_of(i * 256, 256), 256)
            other = st_in[r, :, cols].astype(F32)
            if upper:
                before_ref[:, cols] += before_dec[0:1, cols] * other
            if r < rounds - 1:
                if upper:
                    fresh = total_dec[0:1, cols] * other + total[:, cols]
                else:
                    fresh = dec_in[r, 0:1, cols] * total[:, cols] + other
                total[:, cols] = fresh
                st_out[r, :, cols] = fresh.astype(BF16)

        if upper:
            before_dec[...] *= dec_in[r]
        if r < rounds - 1:
            total_dec[...] *= dec_in[r]
            dec_out[r] = total_dec[...]

    def passing(r):
        bit = (s // 2 ** r) % 2
        partner = s + (1 - 2 * bit) * 2 ** r
        src = tot_ref if r == 0 else st_out.at[r - 1]
        dec = totdec_ref if r == 0 else dec_out.at[r - 1]
        return bit, (
            remote(src, st_in.at[r], st_send.at[r, 0], st_recv.at[r, 0], {"seq": partner}),
            remote(dec, dec_in.at[r], st_send.at[r, 1], st_recv.at[r, 1], {"seq": partner}),
        )

    part_of = s // (n // 4)
    final = rounds - 1

    def onward(own):
        src = st_out.at[final - 1] if own else st_in.at[final]
        dec = dec_out.at[final - 1] if own else dec_in.at[final]
        where = {"seq": (s + n // 4) % n}
        return (
            remote(src, st_in.at[final], st_send.at[final, 0], st_recv.at[final, 0], where),
            remote(dec, dec_in.at[final], st_send.at[final, 1], st_recv.at[final, 1], where),
        )

    def start_round(r):
        if r < final:
            for copy in passing(r)[1]:
                copy.start()
        else:
            @pl.when(part_of == 1)
            def _():
                for copy in onward(True):
                    copy.start()

    def finish_round(r):
        if r < final:
            bit, copies = passing(r)
            for copy in copies:
                copy.wait_recv()

            @pl.when(bit == 1)
            def _():
                combine(r, True)

            @pl.when(bit == 0)
            def _():
                combine(r, False)

            start_round(r + 1)
        else:
            @pl.when(part_of >= 2)
            def _():
                for copy in onward(True):
                    copy.wait_recv()

                @pl.when(part_of == 2)
                def _():
                    for copy in onward(False):
                        copy.start()

                combine(r, True)

    def multiply(u, block):
        tile = min(256, width)

        @pl.loop(0, width // tile)
        def _(i):
            cols = pl.ds(pl.multiple_of(i * tile, tile), tile)
            value = dot(block[...], weight_ref[:, cols]).astype(BF16)
            for q in range(tps):
                part[u, q, :, cols] = value[q * quarter:(q + 1) * quarter]

    def reduction(u, j):
        peer = (t + j) % tps
        return remote(
            part.at[u, peer], red.at[u, j - 1], red_send.at[u, j - 1], red_recv.at[u, j - 1],
            {"tp": peer},
        )

    def begin(u, block):
        multiply(u, block)
        for j in range(1, tps):
            reduction(u, j).start()

    def delivery(u, owner):
        return remote(
            fin.at[u], landed.at[s % per, t], fin_send.at[u], fin_recv.at[s % per, t],
            {"seq": owner, "tp": s // per},
        )

    def close(u, owner):
        for j in range(1, tps):
            reduction(u, j).wait_recv()
        value = part[u, t].astype(F32)
        for j in range(1, tps):
            value = value + red[u, j - 1].astype(F32)
        fin[u] = value.astype(BF16)
        if u:
            delivery(u, owner).start()
        else:
            @pl.when(t == s // per)
            def _():
                pltpu.make_async_copy(
                    fin.at[u], landed.at[s % per, t], fin_recv.at[s % per, t]
                ).start()

            @pl.when(t != s // per)
            def _():
                delivery(u, owner).start()

    x_load = pltpu.make_async_copy(x_hbm, x, load.at[0])
    weight_load = pltpu.make_async_copy(weight_hbm, weight_ref, load.at[1])
    for h in range(2):
        for way in range(2):
            if carries(way, 0, h):
                hop(way, 0, h).start()
    x_load.start()
    weight_load.start()
    total[...] = jnp.zeros_like(total)
    total_dec[...] = jnp.ones_like(total_dec)
    before_ref[...] = jnp.zeros_like(before_ref)
    before_dec[...] = jnp.ones_like(before_dec)
    x_load.wait()

    @pl.loop(0, block_count)
    def _(b):
        block_prepare(
            b, x, dt_ref, rate_ref, b_ref, blocks, lds, ldts, dtts, decs, total, total_dec
        )

    tot_ref[...] = total[...].astype(BF16)
    totdec_ref[...] = total_dec[...]
    start_round(0)
    weight_load.wait()

    def inside(lo, hi):
        if hi > lo:
            @pl.loop(lo, hi)
            def _(u):
                block_inside(
                    u // groups, u % groups, wide, x, b_ref, c_ref, skip_ref,
                    lds, ldts, dtts, diag,
                )

    units = block_count * groups
    slots_left = max(2 * (steps - 1), 1)
    waiting = []
    done = []
    used = 0
    for k in range(steps):
        for h in range(2):
            for way in range(2):
                if carries(way, k, h):
                    hop(way, k, h).wait_recv()
                    if carries(way, k + 1, h):
                        hop(way, k + 1, h).start()
            if k == 0 and h == 0:
                begin(0, mixed_ref)
                waiting = [(0, s)]
            until = min(units, (2 * k + h + 1) * units // slots_left)
            inside(used, until)
            used = until
        fresh = [(1 + 2 * k, member(place - 1 - k))]
        begin(1 + 2 * k, cw.at[k])
        if k < steps - 1:
            begin(2 + 2 * k, ccw.at[k])
            fresh.append((2 + 2 * k, member(place + 1 + k)))
        for u, owner in waiting:
            close(u, owner)
        done += waiting
        waiting = fresh
        if k < rounds and k < steps - 1:
            finish_round(k)
    for r in range(min(steps - 1, rounds), rounds):
        finish_round(r)

    @pl.loop(0, units)
    def _(u):
        block_finish(
            u // groups, u % groups, wide, x, c_ref, before_ref, blocks, decs, lds, diag
        )

    result = pltpu.make_async_copy(x, out_hbm, store.at[0])
    result.start()
    for u, owner in waiting:
        close(u, owner)
    done += waiting

    for g in range(per):
        for q in range(tps):
            remote(
                fin.at[0], landed.at[g, q], fin_send.at[0], fin_recv.at[g, q], {"seq": right}
            ).wait_recv()
            proj_ref[q * quarter:(q + 1) * quarter, g * width:(g + 1) * width] = landed[g, q]

    for k in range(steps):
        for h in range(2):
            for way in range(2):
                if carries(way, k, h):
                    hop(way, k, h).wait_send()
    for u, owner in done:
        for j in range(1, tps):
            reduction(u, j).wait_send()
        if u:
            delivery(u, owner).wait_send()
        else:
            @pl.when(t != s // per)
            def _():
                delivery(u, owner).wait_send()
    for r in range(final):
        for copy in passing(r)[1]:
            copy.wait_send()

    @pl.when(part_of == 1)
    def _():
        for copy in onward(True):
            copy.wait_send()

    @pl.when(part_of == 2)
    def _():
        for copy in onward(False):
            copy.wait_send()

    result.wait()


def layer(n, tps, x, dt, rates, b, c, skip, mixed, weight):
    rows, depth = mixed.shape
    width = weight.shape[1]
    quarter = rows // tps
    steps = n // 2
    per = n // tps
    rounds = n.bit_length() - 1
    length, inner = x.shape
    heads = dt.shape[1]
    blocks = length // SPAN
    groups = heads // GROUP
    state = (STATE, inner)
    dec = (8, inner)
    dma = pltpu.SemaphoreType.DMA
    vmem = pl.BlockSpec(memory_space=pltpu.VMEM)
    hbm = pl.BlockSpec(memory_space=pl.ANY)
    return pl.pallas_call(
        functools.partial(exchange_kernel, n, tps),
        in_specs=[hbm] + [vmem] * 6 + [hbm],
        out_specs=[hbm, vmem],
        out_shape=[
            jax.ShapeDtypeStruct(x.shape, BF16),
            jax.ShapeDtypeStruct((rows, per * width), BF16),
        ],
        scratch_shapes=[
            pltpu.VMEM(x.shape, BF16),
            pltpu.VMEM(weight.shape, BF16),
            pltpu.VMEM((blocks,) + state, F32),
            pltpu.VMEM((blocks, groups, SPAN, GROUP), F32),
            pltpu.VMEM((blocks, heads, SPAN), F32),
            pltpu.VMEM((blocks, heads, SPAN), F32),
            pltpu.VMEM((blocks,) + dec, F32),
            pltpu.VMEM((blocks, groups, SPAN, inner // groups), F32),
            pltpu.VMEM(state, F32),
            pltpu.VMEM(state, BF16),
            pltpu.VMEM(dec, F32),
            pltpu.VMEM((steps, rows, depth), BF16),
            pltpu.VMEM((max(steps - 1, 1), rows, depth), BF16),
            pltpu.VMEM((n, tps, quarter, width), BF16),
            pltpu.VMEM((n, tps - 1, quarter, width), BF16),
            pltpu.VMEM((n, quarter, width), BF16),
            pltpu.VMEM((per, tps, quarter, width), BF16),
            pltpu.VMEM((rounds - 1,) + state, BF16),
            pltpu.VMEM((rounds,) + state, BF16),
            pltpu.VMEM((rounds - 1,) + dec, F32),
            pltpu.VMEM((rounds,) + dec, F32),
            pltpu.VMEM(state, F32),
            pltpu.VMEM(dec, F32),
            pltpu.VMEM(dec, F32),
            dma((2, steps, 2)),
            dma((2, steps, 2)),
            dma((n, tps - 1)),
            dma((n, tps - 1)),
            dma((n,)),
            dma((per, tps)),
            dma((rounds, 2)),
            dma((rounds, 2)),
            dma((2,)),
            dma((1,)),
        ],
        compiler_params=pltpu.CompilerParams(
            has_side_effects=True, vmem_limit_bytes=67_043_328
        ),
        name="layer",
    )(x, dt, rates, b, c, skip, mixed, weight)


def per_device(
    n, tps,
    ssm_inputs,
    step_sizes,
    decay_rates,
    state_inputs,
    state_readout,
    skip_gain,
    mixed_inputs,
    out_weight,
):
    return layer(
        n, tps,
        ssm_inputs, step_sizes, decay_rates[None, :], state_inputs, state_readout,
        jnp.repeat(skip_gain, HEAD_DIM)[None, :], mixed_inputs, out_weight,
    )


def solution(mesh):
    in_specs = (
        P("seq", "tp"),
        P("seq", "tp"),
        P("tp"),
        P("seq", None),
        P("seq", None),
        P("tp"),
        P("seq", "tp"),
        P("tp", "seq"),
    )
    out_specs = (P("seq", "tp"), P("seq", "tp"))
    return jax.shard_map(
        functools.partial(per_device, mesh.shape["seq"], mesh.shape["tp"]),
        mesh=mesh, in_specs=in_specs, out_specs=out_specs, check_vma=False,
    )
```

time: 160 us -> 134 us (0.84)
  Pallas kernels: 151 us -> 124 us
  local copies, waits for them, and re-layouts: 7.34 us -> 9.05 us
    pallas_call x3 -> x1, Pallas kernels: 151 us -> 124 us  [layer(): pl.pallas_call(functools.partial(exchange_kernel, n, tps), in_specs=[hbm]...]
    unnamed x5, local copies, waits for them, and re-layouts: 4.61 us -> 7.65 us
where the time goes in v2:
time: 134 us
  Pallas kernels  124 us (93%)
  local copies, waits for them, and re-layouts  9.05 us (7%)
    pallas_call x1, Pallas kernels, layer(): pl.pallas_call(functools.partial(exchange_kernel, n, tps), in_specs=[hbm]...  124 us
    unnamed x5, local copies, waits for them, and re-layouts  7.65 us

profile of v2, /device:TPU:3, one launch (start us, length us, event | category | flops | bytes accessed | tf_op | source)
XLA Modules:
  0.0 133.7 jit_solution(12283800638252285484)
XLA Ops:
  0.6 0.7 broadcast_in_dim.7
  1.4 0.7 broadcast_in_dim_reshape.3.skip_ref
  2.0 1.9 %copy.10.dt_ref = f32[1024,32]{1,0:T(8,128)} copy(f32[1024,32]{0,1:T(8,128)} %param.9) | data formatting | bytes 262144 | tf_op args[1]
  3.9 124.0 %layer.1 = (bf16[1024,2048]{1,0:T(8,128)(2,1)}, bf16[192,2048]{1,0:T(8,128)(2,1)}) custom-call(bf16[1024,2048]{1,0:T(8,128)(2,1)} %x_hbm.1, f32[1024,32]{1,0:T(8,128)} %copy.10.dt_ref, f32[1,32]{1,0:T(1,128)} %bitcast.1, bf16[1024,128]{1,0:T(8,128)(2,1)} %b_ref.1, bf16[1024,128]{1,0:T(8,128)(2,1)} %c_ref.1, f32[1,2048]{1,0:T(1,128)} %broadcast_in_dim_reshape.3.skip_ref, ...), custom_call_target="tpu_custom_call" | custom-call | tf_op jit(solution)/shard_map/layer/pallas_call | solution.py:433
  128.0 0.0 copy-start
  128.0 4.9 %copy.13 = bf16[1024,2048]{1,0:T(8,128)(2,1)} copy(bf16[1024,2048]{1,0:T(8,128)(2,1)} %get-tuple-element.4) | data formatting | bytes 8388608
  132.8 0.0 copy-done
  132.8 0.9 copy.14
Async XLA Ops:
  128.0 4.9 %copy-start = (bf16[192,2048]{1,0:T(8,128)(2,1)S(1)}, bf16[192,2048]{1,0:T(8,128)(2,1)}, u32[]{:S(2)}) copy-start(bf16[192,2048]{1,0:T(8,128)(2,1)} %get-tuple-element.5) | copy-start | bytes 2359300

commit v3 on v2

--- a/solution.py
+++ b/solution.py
@@ -125,7 +125,7 @@
     out_hbm, proj_ref,
     x, weight_ref, blocks, lds, ldts, dtts, decs, diag, before_ref, tot_ref, totdec_ref,
     cw, ccw, part, red, fin, landed,
-    st_out, st_in, dec_out, dec_in, total, total_dec, before_dec,
+    st_out, st_in, dec_in, total, total_dec, before_dec,
     ring_send, ring_recv, red_send, red_recv, fin_send, fin_recv, st_send, st_recv,
     load, store,
 ):
@@ -146,7 +146,6 @@
     width = weight_ref.shape[1]
     steps = n // 2
     per = n // tps
-    rounds = n.bit_length() - 1
     block_count, groups = lds.shape[0], lds.shape[1]
     wide = x.shape[1] // groups
 
@@ -169,86 +168,83 @@
     def carries(way, k, h):
         return k < steps and (k < steps - 1 or h == way)
 
-    def combine(r, upper):
+    pair, side = s // 2, s % 2
+    pairs = n // 2
+    share = total.shape[1] // 2
+
+    def swap():
+        where = {"seq": s + 1 - 2 * side}
+        return (
+            remote(tot_ref, st_in.at[0], st_send.at[0], st_recv.at[0], where),
+            remote(totdec_ref, dec_in, st_send.at[1], st_recv.at[1], where),
+        )
+
+    def chain():
+        cols = pl.ds(pl.multiple_of(side * share, share), share)
+        return remote(
+            st_out.at[:, cols], st_in.at[1, :, cols], st_send.at[2], st_recv.at[2],
+            {"seq": (s + 2) % n},
+        )
+
+    def mirror():
+        cols = pl.ds(pl.multiple_of(side * share, share), share)
+        part_ref = st_in.at[1, :, cols]
+        return remote(
+            part_ref, part_ref, st_send.at[3], st_recv.at[3], {"seq": s + 1 - 2 * side}
+        )
+
+    def mirrored():
+        cols = pl.ds(pl.multiple_of((1 - side) * share, share), share)
+        part_ref = st_in.at[1, :, cols]
+        return remote(
+            part_ref, part_ref, st_send.at[3], st_recv.at[3], {"seq": s + 1 - 2 * side}
+        )
+
+    def join_pair():
+        for copy in swap():
+            copy.wait_recv()
+        mine = side.astype(F32)
+
         @pl.loop(0, total.shape[1] // 256)
         def _(i):
             cols = pl.ds(pl.multiple_of(i * 256, 256), 256)
-            other = st_in[r, :, cols].astype(F32)
-            if upper:
-                before_ref[:, cols] += before_dec[0:1, cols] * other
-            if r < rounds - 1:
-                if upper:
-                    fresh = total_dec[0:1, cols] * other + total[:, cols]
-                else:
-                    fresh = dec_in[r, 0:1, cols] * total[:, cols] + other
-                total[:, cols] = fresh
-                st_out[r, :, cols] = fresh.astype(BF16)
-
-        if upper:
-            before_dec[...] *= dec_in[r]
-        if r < rounds - 1:
-            total_dec[...] *= dec_in[r]
-            dec_out[r] = total_dec[...]
-
-    def passing(r):
-        bit = (s // 2 ** r) % 2
-        partner = s + (1 - 2 * bit) * 2 ** r
-        src = tot_ref if r == 0 else st_out.at[r - 1]
-        dec = totdec_ref if r == 0 else dec_out.at[r - 1]
-        return bit, (
-            remote(src, st_in.at[r], st_send.at[r, 0], st_recv.at[r, 0], {"seq": partner}),
-            remote(dec, dec_in.at[r], st_send.at[r, 1], st_recv.at[r, 1], {"seq": partner}),
-        )
-
-    part_of = s // (n // 4)
-    final = rounds - 1
-
-    def onward(own):
-        src = st_out.at[final - 1] if own else st_in.at[final]
-        dec = dec_out.at[final - 1] if own else dec_in.at[final]
-        where = {"seq": (s + n // 4) % n}
-        return (
-            remote(src, st_in.at[final], st_send.at[final, 0], st_recv.at[final, 0], where),
-            remote(dec, dec_in.at[final], st_send.at[final, 1], st_recv.at[final, 1], where),
-        )
-
-    def start_round(r):
-        if r < final:
-            for copy in passing(r)[1]:
-                copy.start()
-        else:
-            @pl.when(part_of == 1)
-            def _():
-                for copy in onward(True):
-                    copy.start()
-
-    def finish_round(r):
-        if r < final:
-            bit, copies = passing(r)
-            for copy in copies:
-                copy.wait_recv()
-
-            @pl.when(bit == 1)
-            def _():
-                combine(r, True)
-
-            @pl.when(bit == 0)
-            def _():
-                combine(r, False)
-
-            start_round(r + 1)
-        else:
-            @pl.when(part_of >= 2)
-            def _():
-                for copy in onward(True):
-                    copy.wait_recv()
-
-                @pl.when(part_of == 2)
-                def _():
-                    for copy in onward(False):
-                        copy.start()
-
-                combine(r, True)
+            other = st_in[0, :, cols].astype(F32)
+            own = total[:, cols]
+            before_ref[:, cols] = mine * other
+            upper = total_dec[0:1, cols] * other + own
+            under = dec_in[0:1, cols] * own + other
+            fresh = mine * upper + (1.0 - mine) * under
+            total[:, cols] = fresh
+
+        before_dec[...] = mine * dec_in[...] + (1.0 - mine)
+        total_dec[...] = total_dec[...] * dec_in[...]
+
+        @pl.when(pair == 0)
+        def _():
+            st_out[...] = total[...].astype(BF16)
+            chain().start()
+
+    def link(q):
+        @pl.when(pair == q)
+        def _():
+            chain().wait_recv()
+            if q < pairs - 1:
+                cols = pl.ds(pl.multiple_of(side * share, share), share)
+                st_out[:, cols] = (
+                    total_dec[0:1, cols] * st_in[1, :, cols].astype(F32) + total[:, cols]
+                ).astype(BF16)
+                chain().start()
+            mirror().start()
+
+    def join_all():
+        @pl.when(pair > 0)
+        def _():
+            mirrored().wait_recv()
+
+            @pl.loop(0, total.shape[1] // 256)
+            def _(i):
+                cols = pl.ds(pl.multiple_of(i * 256, 256), 256)
+                before_ref[:, cols] += before_dec[0:1, cols] * st_in[1, :, cols].astype(F32)
 
     def multiply(u, block):
         tile = min(256, width)
@@ -320,7 +316,8 @@
 
     tot_ref[...] = total[...].astype(BF16)
     totdec_ref[...] = total_dec[...]
-    start_round(0)
+    for copy in swap():
+        copy.start()
     weight_load.wait()
 
     def inside(lo, hi):
@@ -347,6 +344,10 @@
             if k == 0 and h == 0:
                 begin(0, mixed_ref)
                 waiting = [(0, s)]
+            if 2 * k + h == 1:
+                join_pair()
+            if 1 <= 2 * k + h - 2 < pairs:
+                link(2 * k + h - 2)
             until = min(units, (2 * k + h + 1) * units // slots_left)
             inside(used, until)
             used = until
@@ -359,10 +360,10 @@
             close(u, owner)
         done += waiting
         waiting = fresh
-        if k < rounds and k < steps - 1:
-            finish_round(k)
-    for r in range(min(steps - 1, rounds), rounds):
-        finish_round(r)
+    for u, owner in waiting:
+        close(u, owner)
+    done += waiting
+    join_all()
 
     @pl.loop(0, units)
     def _(u):
@@ -372,9 +373,6 @@
 
     result = pltpu.make_async_copy(x, out_hbm, store.at[0])
     result.start()
-    for u, owner in waiting:
-        close(u, owner)
-    done += waiting
 
     for g in range(per):
         for q in range(tps):
@@ -397,19 +395,16 @@
             @pl.when(t != s // per)
             def _():
                 delivery(u, owner).wait_send()
-    for r in range(final):
-        for copy in passing(r)[1]:
-            copy.wait_send()
-
-    @pl.when(part_of == 1)
+    for copy in swap():
+        copy.wait_send()
+
+    @pl.when(pair < pairs - 1)
     def _():
-        for copy in onward(True):
-            copy.wait_send()
-
-    @pl.when(part_of == 2)
+        chain().wait_send()
+
+    @pl.when(pair > 0)
     def _():
-        for copy in onward(False):
-            copy.wait_send()
+        mirror().wait_send()
 
     result.wait()
 
@@ -420,7 +415,6 @@
     quarter = rows // tps
     steps = n // 2
     per = n // tps
-    rounds = n.bit_length() - 1
     length, inner = x.shape
     heads = dt.shape[1]
     blocks = length // SPAN
@@ -456,10 +450,9 @@
             pltpu.VMEM((n, tps - 1, quarter, width), BF16),
             pltpu.VMEM((n, quarter, width), BF16),
             pltpu.VMEM((per, tps, quarter, width), BF16),
-            pltpu.VMEM((rounds - 1,) + state, BF16),
-            pltpu.VMEM((rounds,) + state, BF16),
-            pltpu.VMEM((rounds - 1,) + dec, F32),
-            pltpu.VMEM((rounds,) + dec, F32),
+            pltpu.VMEM(state, BF16),
+            pltpu.VMEM((2,) + state, BF16),
+            pltpu.VMEM(dec, F32),
             pltpu.VMEM(state, F32),
             pltpu.VMEM(dec, F32),
             pltpu.VMEM(dec, F32),
@@ -469,8 +462,8 @@
             dma((n, tps - 1)),
             dma((n,)),
             dma((per, tps)),
-            dma((rounds, 2)),
-            dma((rounds, 2)),
+            dma((4,)),
+            dma((4,)),
             dma((2,)),
             dma((1,)),
         ],

time: 134 us -> 121 us (0.903)
  Pallas kernels: 124 us -> 111 us
    pallas_call x1, Pallas kernels: 124 us -> 111 us  [layer(): pl.pallas_call(functools.partial(exchange_kernel, n, tps), in_specs=[hbm]...]
where the time goes in v3:
time: 121 us
  Pallas kernels  111 us (92%)
  local copies, waits for them, and re-layouts  9.05 us (7%)
    pallas_call x1, Pallas kernels, layer(): pl.pallas_call(functools.partial(exchange_kernel, n, tps), in_specs=[hbm]...  111 us
    unnamed x5, local copies, waits for them, and re-layouts  7.65 us

profile of v3, /device:TPU:3, one launch (start us, length us, event | category | flops | bytes accessed | tf_op | source)
XLA Modules:
  0.0 120.7 jit_solution(4226226445935188922)
XLA Ops:
  0.6 0.7 broadcast_in_dim.7
  1.4 0.7 broadcast_in_dim_reshape.3.skip_ref
  2.0 1.9 %copy.10.dt_ref = f32[1024,32]{1,0:T(8,128)} copy(f32[1024,32]{0,1:T(8,128)} %param.9) | data formatting | bytes 262144 | tf_op args[1]
  3.9 111.0 %layer.1 = (bf16[1024,2048]{1,0:T(8,128)(2,1)}, bf16[192,2048]{1,0:T(8,128)(2,1)}) custom-call(bf16[1024,2048]{1,0:T(8,128)(2,1)} %x_hbm.1, f32[1024,32]{1,0:T(8,128)} %copy.10.dt_ref, f32[1,32]{1,0:T(1,128)} %bitcast.1, bf16[1024,128]{1,0:T(8,128)(2,1)} %b_ref.1, bf16[1024,128]{1,0:T(8,128)(2,1)} %c_ref.1, f32[1,2048]{1,0:T(1,128)} %broadcast_in_dim_reshape.3.skip_ref, ...), custom_call_target="tpu_custom_call" | custom-call | tf_op jit(solution)/shard_map/layer/pallas_call | solution.py:427
  114.9 0.0 copy-start
  114.9 4.9 %copy.13 = bf16[1024,2048]{1,0:T(8,128)(2,1)} copy(bf16[1024,2048]{1,0:T(8,128)(2,1)} %get-tuple-element.4) | data formatting | bytes 8388608
  119.8 0.0 copy-done
  119.8 0.9 copy.14
Async XLA Ops:
  114.9 4.9 %copy-start = (bf16[192,2048]{1,0:T(8,128)(2,1)S(1)}, bf16[192,2048]{1,0:T(8,128)(2,1)}, u32[]{:S(2)}) copy-start(bf16[192,2048]{1,0:T(8,128)(2,1)} %get-tuple-element.5) | copy-start | bytes 2359300
